TPU v7x, 16 devices: a whole 2x2x2 slice. The times are simulated.
16 devices in a mesh: data: 16 (over z, y, x, core).
Axes of the slice: x: 2, y: 2, z: 2, core: 2. Of those that a mesh axis runs over, the one named last changes fastest.
Arguments:
- w_in: float32 [16, 512, 2048], replicated
- w_out: float32 [16, 2048, 512], replicated
- mom_in: float32 [16, 512, 2048], replicated
- mom_out: float32 [16, 2048, 512], replicated
- x_first: bfloat16 [8192, 512], P('data')
- y_first: bfloat16 [8192, 512], P('data')
- x_second: bfloat16 [8192, 512], P('data')
- y_second: bfloat16 [8192, 512], P('data')
Outputs:
- output 1: float32 [16, 512, 2048], replicated
- output 2: float32 [16, 2048, 512], replicated
- output 3: float32 [16, 512, 2048], replicated
- output 4: float32 [16, 2048, 512], replicated
- output 5: float32 [8192], P('data')
- output 6: float32 [8192, 512], P('data')
All inputs are finite; a program needn't handle non-finite values.
Results may differ from a plain program's by a relative error of at most 0.00755277.
Values are sent between devices in bfloat16 or wider.
A program may use at most 2.25 GiB of HBM per device.

v0:
```python
import jax
import jax.numpy as jnp
from jax import lax
from jax.sharding import PartitionSpec as P

LR_SCALE = 1.0
MOMENTUM = 0.9
ROW_CONTRACT = (((0,), (0,)), ((), ()))
COL_CONTRACT = (((1,), (1,)), ((), ()))


def forward_stack(w_in_list, w_out_list, h_cur):
    saved_acts = []
    for w_in_l, w_out_l in zip(w_in_list, w_out_list):
        h_bf = h_cur.astype(jnp.bfloat16)
        pre_act = jnp.dot(h_bf, w_in_l, preferred_element_type=jnp.float32)
        act_bf = jax.nn.gelu(pre_act).astype(jnp.bfloat16)
        h_cur = h_cur + jnp.dot(act_bf, w_out_l, preferred_element_type=jnp.float32)
        saved_acts.append((h_bf, pre_act, act_bf))
    return h_cur, saved_acts


def layer_backward(w_in_l, w_out_l, saved_layer, err_row, need_err):
    h_bf, pre_act, act_bf = saved_layer
    err_bf = err_row.astype(jnp.bfloat16)
    grad_out = lax.dot_general(act_bf, err_bf, ROW_CONTRACT, preferred_element_type=jnp.float32)
    d_act = lax.dot_general(err_bf, w_out_l, COL_CONTRACT, preferred_element_type=jnp.float32)
    d_pre = jax.vjp(jax.nn.gelu, pre_act)[1](d_act)[0].astype(jnp.bfloat16)
    grad_in = lax.dot_general(h_bf, d_pre, ROW_CONTRACT, preferred_element_type=jnp.float32)
    if need_err:
        err_row = err_row + lax.dot_general(d_pre, w_in_l, COL_CONTRACT, preferred_element_type=jnp.float32)
    return grad_in.astype(jnp.bfloat16), grad_out.astype(jnp.bfloat16), err_row


def apply_update(weights, moments, grad_sum, step_size):
    mom_new = MOMENTUM * moments + grad_sum.astype(jnp.float32)
    return weights - step_size * mom_new, mom_new


def solution(mesh):
    groups = mesh.shape["data"]
    rows_spec = P("data", None)

    def local_steps(w_in, w_out, mom_in, mom_out, x_first, y_first, x_second, y_second):
        layers = w_in.shape[0]
        tok_local, model_dim = x_first.shape
        step_size = LR_SCALE / layers
        w_in_list = [w_in[layer_idx].astype(jnp.bfloat16) for layer_idx in range(layers)]
        w_out_list = [w_out[layer_idx].astype(jnp.bfloat16) for layer_idx in range(layers)]
        h_last, saved_acts = forward_stack(w_in_list, w_out_list, x_first.astype(jnp.float32))
        err_row = (h_last - y_first.astype(jnp.float32)) * (1.0 / (tok_local * groups * model_dim))
        sums_in = [None] * layers
        sums_out = [None] * layers
        for layer_idx in reversed(range(layers)):
            grad_in, grad_out, err_row = layer_backward(w_in_list[layer_idx], w_out_list[layer_idx], saved_acts[layer_idx], err_row, layer_idx > 0)
            sums_in[layer_idx], sums_out[layer_idx] = lax.psum((grad_in, grad_out), "data")
        w_in_new, mom_in_new = apply_update(w_in, mom_in, jnp.stack(sums_in), step_size)
        w_out_new, mom_out_new = apply_update(w_out, mom_out, jnp.stack(sums_out), step_size)
        new_in_list = [w_in_new[layer_idx].astype(jnp.bfloat16) for layer_idx in range(layers)]
        new_out_list = [w_out_new[layer_idx].astype(jnp.bfloat16) for layer_idx in range(layers)]
        h_next, unused = forward_stack(new_in_list, new_out_list, x_second.astype(jnp.float32))
        row_diff = h_next - y_second.astype(jnp.float32)
        loss_rows = jnp.sum(row_diff * row_diff, axis=-1) / (2 * model_dim)
        return w_in_new, w_out_new, mom_in_new, mom_out_new, loss_rows, h_next

    return jax.shard_map(local_steps, mesh=mesh, in_specs=(P(), P(), P(), P(), rows_spec, rows_spec, rows_spec, rows_spec), out_specs=(P(), P(), P(), P(), P("data"), rows_spec), check_vma=False)
```

profile of v0, /device:TPU:0, one launch (start us, length us, event | category | flops | bytes accessed | tf_op | source)
XLA Modules:
  0.0 1826.4 jit_solution(12694516967739557148)
XLA Ops:
  7.2 32.4 %convert.72 = bf16[16,512,2048]{2,1,0:T(8,128)(2,1)} convert(f32[16,512,2048]{2,1,0:T(8,128)} %param.8) | non-fusion elementwise | flops 16777216 | bytes 100663296 | tf_op jit(solution)/shard_map/convert.63
  39.6 32.4 %convert.73 = bf16[16,2048,512]{2,1,0:T(8,128)(2,1)} convert(f32[16,2048,512]{2,1,0:T(8,128)} %param.9) | non-fusion elementwise | flops 16777216 | bytes 100663296 | tf_op jit(solution)/shard_map/convert.62
  84.4 5.0 fusion.397
  91.7 4.6 fusion.395
  97.5 4.6 fusion.393
  103.4 5.1 fusion.391
  109.8 4.6 fusion.389
  115.7 4.6 fusion.387
  121.6 4.6 fusion.385
  127.5 4.6 fusion.383
  133.4 4.8 fusion.381
  143.8 4.6 fusion.377
  151.7 4.3 fusion.375
  157.3 4.6 fusion.373
  165.2 4.6 fusion.371
  172.0 5.9 fusion.369
  177.9 4.5 fusion.271
  182.4 7.7 fusion.111
  190.1 4.3 fusion.370
  194.4 4.4 fusion.270
  198.8 8.1 fusion.104
  207.0 4.3 fusion.372
  211.2 4.5 fusion.269
  215.7 7.7 fusion.97
  227.7 4.4 fusion.268
  232.1 7.9 fusion.90
  240.1 4.3 fusion.376
  244.3 4.5 fusion.267
  248.8 7.8 fusion.83
  263.9 6.7 fusion.76
  278.2 6.5 fusion.69
  292.2 6.9 fusion.62
  306.6 6.5 fusion.55
  320.7 6.7 fusion.48
  334.8 6.5 fusion.41
  348.8 6.8 fusion.34
  363.1 6.5 fusion.27
  377.2 6.9 fusion.20
  391.7 6.6 fusion.13
  398.2 4.7 fusion.255
  445.1 7.1 fusion.240
  452.3 62.5 %copy.30 = f32[16,512,2048]{1,2,0:T(8,128)} copy(f32[16,512,2048]{2,1,0:T(8,128)} %param.8) | data formatting | bytes 134217728 | tf_op args[0]
  514.8 62.9 %copy.14 = f32[16,512,2048]{1,2,0:T(8,128)} copy(f32[16,512,2048]{2,1,0:T(8,128)} %param.10) | data formatting | bytes 134217728 | tf_op args[2]
  579.8 772.2 %all-reduce.3.cloned.1.call-done = (bf16[1,512,2048]{1,2,0:T(8,128)(2,1)}, bf16[1,512,2048]{1,2,0:T(8,128)(2,1)}, bf16[1,512,2048]{1,2,0:T(8,128)(2,1)}, bf16[1,...) async-done(((bf16[1,512,2048]{1,2,0:T(8,128)(2,1)}, ...) | async-done | bytes 67108880 | tf_op jit(solution)/shard_map/psum | solution.py:56
  1378.7 105.0 %fusion.578 = (bf16[16,2048,512]{2,1,0:T(8,128)(2,1)}, f32[16,2048,512]{2,1,0:T(8,128)}, f32[16,2048,512]{2,1,0:T(8,128)}) fusion(f32[16,2048,512]{2,1,0:T(8,128)} %param.9, bf16[16,2048,512]{2,1,0:T(8,128)(2,1)} %constant_dynamic-update-slice_fusion.16, f32[16,2048,512]{2,1,0:T(8,128)} %param.11), kind=kLoop, calls=%fused_computation.760 | loop fusion | flops 100663296 | bytes 335544320 | tf_op jit(solution)/shard_map/convert.30
  1506.7 105.6 %fusion.577 = (bf16[16,512,2048]{1,2,0:T(8,128)(2,1)}, f32[16,512,2048]{1,2,0:T(8,128)}, f32[16,512,2048]{1,2,0:T(8,128)}) fusion(f32[16,512,2048]{1,2,0:T(8,128)} %copy.30, bf16[16,512,2048]{1,2,0:T(8,128)(2,1)} %constant_dynamic-update-slice_fusion, f32[16,512,2048]{1,2,0:T(8,128)} %copy.14), kind=kLoop, calls=%fused_computation.759 | loop fusion | flops 100663296 | bytes 335544320 | tf_op jit(solution)/shard_map/convert.31
  1612.3 4.9 fusion.400
  1617.2 5.0 fusion.401
  1622.2 5.0 fusion.402
  1627.2 5.0 fusion.403
  1632.1 5.2 fusion.404
  1637.3 4.9 fusion.405
  1642.3 5.0 fusion.406
  1647.2 5.0 fusion.407
  1652.2 5.4 fusion.408
  1657.6 5.0 fusion.409
  1662.5 5.0 fusion.410
  1667.5 5.0 fusion.411
  1672.4 5.1 fusion.412
  1677.6 5.0 fusion.413
  1682.6 5.0 fusion.414
  1687.6 5.0 multiply_reduce_fusion
  1694.5 62.5 %copy.34 = f32[16,512,2048]{2,1,0:T(8,128)} copy(f32[16,512,2048]{1,2,0:T(8,128)} %get-tuple-element.45) | data formatting | bytes 134217728
  1757.0 62.5 %copy.35 = f32[16,512,2048]{2,1,0:T(8,128)} copy(f32[16,512,2048]{1,2,0:T(8,128)} %get-tuple-element.46) | data formatting | bytes 134217728
  (350 shorter events, 213.9 us)
Async XLA Ops:
  7.2 1344.8 %all-reduce.3.cloned.1.call-start = ((), (), s32[]{:S(2)}) async-start(), calls=%async_computation | async-start | bytes 134217728 | tf_op jit(solution)/shard_map/psum | solution.py:56
  39.6 32.4 %copy-start.92 = (bf16[512,512]{1,0:T(8,128)(2,1)S(1)}, bf16[512,512]{1,0:T(8,128)(2,1)}, u32[]{:S(2)}) copy-start(bf16[512,512]{1,0:T(8,128)(2,1)} %param.12) | copy-start | bytes 1572868
  72.0 17.3 slice-start
  77.1 12.3 slice-start.1
  77.1 12.3 slice-start.2
  77.1 12.3 slice-start.3
  80.3 4.0 copy-start.27
  80.3 9.1 slice-start.4
  80.3 9.1 slice-start.5
  84.3 5.0 copy-start
  84.4 5.1 slice-start.6
  84.4 6.0 slice-start.7
  91.6 4.6 copy-start.2
  97.5 4.6 copy-start.4
  103.4 5.1 copy-start.6
  109.8 4.6 copy-start.8
  115.7 4.6 copy-start.10
  121.6 4.6 copy-start.12
  127.5 4.6 copy-start.14
  133.4 4.8 copy-start.16
  143.8 4.6 copy-start.18
  148.4 3.3 copy-start.49
  157.3 4.6 copy-start.21
  161.9 3.3 copy-start.53
  172.0 5.9 copy-start.24
  190.1 4.3 copy-start.23
  207.0 4.3 copy-start.22
  223.4 4.3 copy-start.20
  240.1 4.3 copy-start.19
  270.7 4.3 copy-start.17
  284.7 4.3 copy-start.15
  299.1 4.3 copy-start.13
  313.2 4.3 copy-start.11
  327.3 4.3 copy-start.9
  341.4 4.3 copy-start.7
  355.6 4.3 copy-start.5
  369.6 4.4 copy-start.3
  384.1 4.3 copy-start.1
  398.2 4.7 copy-start.54
  398.2 4.7 copy-start.95
  441.9 3.2 copy-start.93
  514.8 63.0 %copy-start.88 = (bf16[512,512]{1,0:T(8,128)(2,1)S(1)}, bf16[512,512]{1,0:T(8,128)(2,1)}, u32[]{:S(2)}) copy-start(bf16[512,512]{1,0:T(8,128)(2,1)} %param.14) | copy-start | bytes 1572868
  514.8 64.0 %copy-start.87 = (bf16[512,512]{1,0:T(8,128)(2,1)S(1)}, bf16[512,512]{1,0:T(8,128)(2,1)}, u32[]{:S(2)}) copy-start(bf16[512,512]{1,0:T(8,128)(2,1)} %param.15) | copy-start | bytes 1572868
  1351.9 3.2 copy-start.86
  1351.9 4.7 copy-start.85
  1356.6 3.0 copy-start.83
  1358.1 3.0 copy-start.82
  1359.6 3.0 copy-start.81
  1368.4 3.0 copy-start.75
  1369.9 3.0 copy-start.74
  1371.3 3.0 copy-start.73
  1372.8 2.9 copy-start.72
  1378.7 105.0 %copy-start.70 = (bf16[1,512,2048]{1,2,0:T(8,128)(2,1)S(1)}, bf16[1,512,2048]{1,2,0:T(8,128)(2,1)}, u32[]{:S(2)}) copy-start(bf16[1,512,2048]{1,2,0:T(8,128)(2,1)} %get-tuple-element.13) | copy-start | bytes 6291460
  1483.7 3.8 copy-start.68
  1486.1 3.0 copy-start.67
  1487.6 2.9 copy-start.66
  1489.1 2.9 copy-start.65
  1496.4 3.0 copy-start.60
  1497.8 3.0 copy-start.59
  1499.3 2.9 copy-start.58
  1500.8 2.9 copy-start.57
  1506.7 105.6 %copy-start.89 = (bf16[512,512]{1,0:T(8,128)(2,1)S(1)}, bf16[512,512]{1,0:T(8,128)(2,1)}, u32[]{:S(2)}) copy-start(bf16[512,512]{1,0:T(8,128)(2,1)} %param.14) | copy-start | bytes 1572868
  1506.7 105.6 %copy-start.91 = (bf16[512,512]{0,1:T(8,128)(2,1)S(1)}, bf16[512,512]{0,1:T(8,128)(2,1)}, u32[]{:S(2)}) copy-start(bf16[512,512]{0,1:T(8,128)(2,1)} %copy.31) | copy-start | bytes 1572868
  1682.5 5.0 copy-start.90
  (65 other events, 139.5 us)
Sparse Core Ops, SparseCore 0:
  452.4 899.4 all-reduce.2
where the time goes:
time: 1840 us; the launch traced here: 1830 us
  waiting for transfers between devices  772 us (42%)
  matrix products  445 us (24%)
  local copies, waits for them, and re-layouts  317 us (17%)
  other arithmetic  276 us (15%)
    psum x1, waiting for transfers between devices, local_steps(): lax.psum((grad_in, grad_out), 'data')  772 us
    unnamed x293, local copies, waits for them, and re-layouts  314 us
    another operation x4, other arithmetic  275 us
    dot_general x32, matrix products, forward_stack(): h_cur = h_cur + jnp.dot(act_bf, w_out_l, preferred_element_type=jnp.float32)  153 us
    dot_general x15, matrix products, layer_backward(): lax.dot_general(err_bf, w_out_l, COL_CONTRACT, preferred_element_type=jnp...  106 us
    dot_general x16, matrix products, layer_backward(): lax.dot_general(act_bf, err_bf, ROW_CONTRACT, preferred_element_type=jnp....  57.8 us
    dot_general x15, matrix products, layer_backward(): lax.dot_general(d_pre, w_in_l, COL_CONTRACT, preferred_element_type=jnp.f...  51 us
    dot_general x16, matrix products, layer_backward(): lax.dot_general(h_bf, d_pre, ROW_CONTRACT, preferred_element_type=jnp.flo...  49.3 us
  transfers between devices with their start and end apart: 1, of which 1 were waited for; matrix products, arithmetic and copies ran while one was open for 7% of the time, Pallas kernels for 0%

commit v1 on v0

v1 whole, which is shorter than its diff:
```python
import functools

import jax
import jax.numpy as jnp
from jax import lax
from jax.experimental import pallas as pl
from jax.experimental.pallas import tpu as pltpu
from jax.sharding import PartitionSpec as P

MESH = pl.DeviceIdType.MESH
BF = jnp.bfloat16
F32 = jnp.float32
LAYERS, DIM, HID, ROWS = 16, 512, 2048, 512
TILE = 512
PER = HID // TILE
UNITS = LAYERS * PER
STEP = 1.0 / LAYERS
MU = 0.9
C0 = 0.7978845608028654
C1 = C0 * 0.044715
BLOCK = (160, 160, 192)
START = (0, 160, 320)
HALF = (80, 80, 96)
HSTART = (0, 80, 160)
RING = 8
CHUNKS = ((0, 8), (8, 13), (13, 16))
VMEM_LIMIT = 60 * 2**20


def dot(a, b, ca=1, cb=0):
    return lax.dot_general(a, b, (((ca,), (cb,)), ((), ())), preferred_element_type=F32)


def gelu(z):
    t = jnp.tanh(z * (C0 + C1 * (z * z)))
    return z * (0.5 * t + 0.5)


def gelu_both(z):
    z2 = z * z
    t = jnp.tanh(z * (C0 + C1 * z2))
    cdf = 0.5 * t + 0.5
    return z * cdf, cdf + (0.5 * z) * ((1.0 - t * t) * (C0 + (3.0 * C1) * z2))


def axis_peer(me, order):
    stride = order * order + order + 2
    bit = lax.rem(lax.div(me, stride), 2)
    return bit, me + (1 - 2 * bit) * stride


def fwd_kernel(tiles, x_ref, w1_ref, w2_ref, hs_ref, hl_ref, h_s, hb_s):
    i = pl.program_id(0)
    j = lax.rem(i, tiles)

    @pl.when(i == 0)
    def _():
        h_s[...] = x_ref[...].astype(F32)

    @pl.when(j == 0)
    def _():
        hb_s[...] = h_s[...].astype(BF)
        hs_ref[0] = hb_s[...]

    z = dot(hb_s[...], w1_ref[0].astype(BF))
    h_s[...] += dot(gelu(z).astype(BF), w2_ref[0].astype(BF))

    @pl.when(i == LAYERS * tiles - 1)
    def _():
        hl_ref[...] = h_s[...]


def forward_first(x, w_in, w_out):
    tiles = 2
    th = HID // tiles
    full = pl.BlockSpec((ROWS, DIM), lambda i: (0, 0))
    return pl.pallas_call(
        functools.partial(fwd_kernel, tiles),
        grid=(LAYERS * tiles,),
        in_specs=[
            full,
            pl.BlockSpec((1, DIM, th), lambda i: (i // tiles, 0, i % tiles)),
            pl.BlockSpec((1, th, DIM), lambda i: (i // tiles, i % tiles, 0)),
        ],
        out_specs=[pl.BlockSpec((1, ROWS, DIM), lambda i: (i // tiles, 0, 0)), full],
        out_shape=[
            jax.ShapeDtypeStruct((LAYERS, ROWS, DIM), BF),
            jax.ShapeDtypeStruct((ROWS, DIM), F32),
        ],
        scratch_shapes=[pltpu.VMEM((ROWS, DIM), F32), pltpu.VMEM((ROWS, DIM), BF)],
        compiler_params=pltpu.CompilerParams(vmem_limit_bytes=VMEM_LIMIT),
        name="fwd_first",
    )(x, w_in, w_out)


def bwd_kernel(
    inv, w1_ref, w2_ref, hb_ref, hl_ref, y_ref, out_ref,
    e_s, eb_s, ht_s, gst, rb, acc, rv1, rv2, rv3,
    s0, r0, s1, r1, s2, r2, s3, r3,
):
    i = pl.program_id(0)
    me = lax.axis_index("data")
    core = lax.rem(me, 2)
    sib = me + 1 - 2 * core

    @pl.when(i == 0)
    def _():
        bar = pltpu.get_barrier_semaphore()
        pl.semaphore_signal(bar, inc=1, device_id=(sib,), device_id_type=MESH)
        for a in range(3):
            pl.semaphore_signal(bar, inc=1, device_id=(axis_peer(me, a)[1],), device_id_type=MESH)
        pl.semaphore_wait(bar, 4)

    def core_copy(u):
        return pltpu.make_async_remote_copy(
            src_ref=gst.at[lax.rem(u, 4), 1 - core], dst_ref=rb.at[lax.rem(u, RING)],
            send_sem=s0.at[lax.rem(u, 4)], recv_sem=r0.at[lax.rem(u, RING)],
            device_id=(sib,), device_id_type=MESH)

    def geometry(u, k):
        rot = lax.rem(u, 3)
        peers = [axis_peer(me, lax.rem(rot + k + p, 3)) for p in range(3)]
        return [b for b, _ in peers], [n for _, n in peers]

    def rows_of(k, bit):
        return pl.ds(pl.multiple_of(START[k] + bit * HALF[k], 16), HALF[k])

    def cols_of(start, size):
        return pl.ds(pl.multiple_of(start, 128), size)

    def stage_copy(u, k, p):
        bits, peers = geometry(u, k)
        slot = lax.rem(u, RING)
        hs = pl.ds(HSTART[k], HALF[k])
        if p == 0:
            src, dst = acc.at[slot, rows_of(k, 1 - bits[0])], rv1.at[slot, hs]
        elif p == 1:
            src, dst = acc.at[slot, rows_of(k, bits[0]), cols_of((1 - bits[1]) * 256, 256)], rv2.at[slot, hs]
        else:
            src = acc.at[slot, rows_of(k, bits[0]), cols_of(bits[1] * 256 + (1 - bits[2]) * 128, 128)]
            dst = rv3.at[slot, hs]
        ss, rs = ((s1, r1), (s2, r2), (s3, r3))[p]
        return pltpu.make_async_remote_copy(
            src_ref=src, dst_ref=dst, send_sem=ss.at[lax.rem(u, 4), k], recv_sem=rs.at[slot, k],
            device_id=(peers[p],), device_id_type=MESH)

    def add(a, b):
        return (a.astype(F32) + b.astype(F32)).astype(BF)

    @pl.when(i >= 8)
    def _():
        u = i - 8
        slot = lax.rem(u, RING)
        for k in range(3):
            stage_copy(u, k, 2).wait()
        for k in range(3):
            bits, _ = geometry(u, k)
            hs = pl.ds(HSTART[k], HALF[k])
            out_ref[0, hs, :] = add(acc[slot, rows_of(k, bits[0]), cols_of(bits[1] * 256 + bits[2] * 128, 128)], rv3[slot, hs, :])

    @pl.when((i >= 6) & (i < UNITS + 6))
    def _():
        u = i - 6
        slot = lax.rem(u, RING)
        for k in range(3):
            stage_copy(u, k, 1).wait()
        for k in range(3):
            bits, _ = geometry(u, k)
            hs = pl.ds(HSTART[k], HALF[k])
            idx = (slot, rows_of(k, bits[0]), cols_of(bits[1] * 256, 256))
            acc[idx] = add(acc[idx], rv2[slot, hs, :])
        for k in range(3):
            stage_copy(u, k, 2).start()

    @pl.when((i >= 4) & (i < UNITS + 4))
    def _():
        u = i - 4
        slot = lax.rem(u, RING)
        for k in range(3):
            stage_copy(u, k, 0).wait()
        for k in range(3):
            bits, _ = geometry(u, k)
            hs = pl.ds(HSTART[k], HALF[k])
            idx = (slot, rows_of(k, bits[0]), pl.ds(0, DIM))
            acc[idx] = add(acc[idx], rv1[slot, hs, :])
        for k in range(3):
            stage_copy(u, k, 1).start()

    @pl.when((i >= 2) & (i < UNITS + 2))
    def _():
        u = i - 2
        slot = lax.rem(u, RING)
        core_copy(u).wait()
        acc[slot] = add(gst[lax.rem(u, 4), core], rb[slot])
        for k in range(3):
            stage_copy(u, k, 0).start()

    @pl.when(i == 0)
    def _():
        e_s[...] = (hl_ref[...] - y_ref[...].astype(F32)) * inv

    @pl.when(i < UNITS)
    def _():
        @pl.when(lax.rem(i, PER) == 0)
        def _():
            eb_s[...] = e_s[...].astype(BF)
            ht_s[...] = hb_ref[0].T

        g = lax.rem(i, 4)
        eb = eb_s[...]
        w1 = w1_ref[0].astype(BF)
        w2 = w2_ref[0].astype(BF)
        z = dot(hb_ref[0], w1)
        q = dot(eb, w2, 1, 1)
        a, da = gelu_both(z)
        s = (da * q).astype(BF)
        gst[g, 1] = dot(a.astype(BF).T, eb).astype(BF)
        gst[g, 0] = dot(ht_s[...], s).astype(BF)
        e_s[...] += dot(s, w1, 1, 1)
        core_copy(i).start()


def backward_scatter(w_in, w_out, hs, hl, y, inv):
    last = UNITS - 1

    def layer(i):
        return LAYERS - 1 - jnp.minimum(i, last) // PER

    full = pl.BlockSpec((ROWS, DIM), lambda i: (0, 0))
    dma = pltpu.SemaphoreType.DMA
    return pl.pallas_call(
        functools.partial(bwd_kernel, inv),
        grid=(UNITS + 8,),
        in_specs=[
            pl.BlockSpec((1, DIM, TILE), lambda i: (layer(i), 0, jnp.minimum(i, last) % PER)),
            pl.BlockSpec((1, TILE, DIM), lambda i: (layer(i), jnp.minimum(i, last) % PER, 0)),
            pl.BlockSpec((1, ROWS, DIM), lambda i: (layer(i), 0, 0)),
            full, full,
        ],
        out_specs=pl.BlockSpec((1, 256, 128), lambda i: (jnp.maximum(i - 8, 0), 0, 0)),
        out_shape=jax.ShapeDtypeStruct((UNITS, 256, 128), BF),
        scratch_shapes=[
            pltpu.VMEM((ROWS, DIM), F32), pltpu.VMEM((ROWS, DIM), BF), pltpu.VMEM((DIM, ROWS), BF),
            pltpu.VMEM((4, 2, 512, 512), BF), pltpu.VMEM((RING, 512, 512), BF), pltpu.VMEM((RING, 512, 512), BF),
            pltpu.VMEM((RING, 256, 512), BF), pltpu.VMEM((RING, 256, 256), BF), pltpu.VMEM((RING, 256, 128), BF),
            dma((4,)), dma((RING,)), dma((4, 3)), dma((RING, 3)), dma((4, 3)), dma((RING, 3)), dma((4, 3)), dma((RING, 3)),
        ],
        compiler_params=pltpu.CompilerParams(
            vmem_limit_bytes=VMEM_LIMIT, collective_id=0, has_side_effects=True),
        name="bwd_scatter",
    )(w_in, w_out, hs, hl, y)


def upd_kernel(lo, hi, nalias, h_ref, g_ref, w1_ref, w2_ref, m1_ref, m2_ref, *rest):
    w1o, w2o, m1o, m2o, ho_ref, h_s, hb_s = rest[nalias:]
    i = pl.program_id(0)
    layer = lo + i // PER
    rot = lax.rem((LAYERS - 1 - layer) * PER + lax.rem(i, PER), 3)

    @pl.when(i == 0)
    def _():
        h_s[...] = h_ref[...].astype(F32)

    @pl.when(lax.rem(i, PER) == 0)
    def _():
        hb_s[...] = h_s[...].astype(BF)

    def chip(q, _):
        for k in range(3):
            bits = []
            for p in range(3):
                a = lax.rem(rot + k + p, 3)
                stride = lax.div(a * a + a + 2, 2)
                bits.append(lax.rem(lax.div(q, stride), 2))
            rows = pl.ds(pl.multiple_of(START[k] + bits[0] * HALF[k], 16), HALF[k])
            cols = pl.ds(pl.multiple_of(bits[1] * 256 + bits[2] * 128, 128), 128)
            for c, (w, m, wo, mo) in enumerate(((w1_ref, m1_ref, w1o, m1o), (w2_ref, m2_ref, w2o, m2o))):
                g = g_ref[2 * q + c, 0, pl.ds(HSTART[k], HALF[k]), :].astype(F32)
                mn = MU * m[0, rows, cols] + g
                mo[0, rows, cols] = mn
                wo[0, rows, cols] = w[0, rows, cols] - STEP * mn
        return 0

    lax.fori_loop(0, 8, chip, 0)
    z = dot(hb_s[...], w1o[0].astype(BF))
    h_s[...] += dot(gelu(z).astype(BF), w2o[0].astype(BF))

    @pl.when(i == (hi - lo) * PER - 1)
    def _():
        ho_ref[...] = h_s[...]


def update_forward(lo, hi, h, g, weights, prev):
    n = (hi - lo) * PER

    def in_map(i):
        return (lo + i // PER, 0, i % PER)

    def out_map(i):
        return (lo + i // PER, i % PER, 0)

    b1 = pl.BlockSpec((1, DIM, TILE), in_map)
    b2 = pl.BlockSpec((1, TILE, DIM), out_map)
    full = pl.BlockSpec((ROWS, DIM), lambda i: (0, 0))
    gspec = pl.BlockSpec((16, 1, 256, 128), lambda i: (0, (hi - lo - 1 - i // PER) * PER + i % PER, 0, 0))
    nalias = len(prev)
    s1 = jax.ShapeDtypeStruct((LAYERS, DIM, HID), F32)
    s2 = jax.ShapeDtypeStruct((LAYERS, HID, DIM), F32)
    return pl.pallas_call(
        functools.partial(upd_kernel, lo, hi, nalias),
        grid=(n,),
        in_specs=[full, gspec, b1, b2, b1, b2] + [pl.BlockSpec(memory_space=pl.ANY)] * nalias,
        out_specs=[b1, b2, b1, b2, full],
        out_shape=[s1, s2, s1, s2, jax.ShapeDtypeStruct((ROWS, DIM), F32)],
        input_output_aliases={6 + a: a for a in range(nalias)},
        scratch_shapes=[pltpu.VMEM((ROWS, DIM), F32), pltpu.VMEM((ROWS, DIM), BF)],
        compiler_params=pltpu.CompilerParams(vmem_limit_bytes=VMEM_LIMIT),
        cost_estimate=pl.CostEstimate(flops=n * 4 * 512**3, bytes_accessed=n * 9 * 2**20, transcendentals=0),
        name="upd_fwd",
    )(h, g, *weights, *prev)


def solution(mesh):
    groups = mesh.shape["data"]
    rows_spec = P("data", None)

    def local_steps(w_in, w_out, mom_in, mom_out, x_first, y_first, x_second, y_second):
        hs, hl = forward_first(x_first, w_in, w_out)
        shards = backward_scatter(w_in, w_out, hs, hl, y_first, 1.0 / (ROWS * groups * DIM))
        gathered = []
        for lo, hi in CHUNKS:
            part = shards[(LAYERS - hi) * PER:(LAYERS - lo) * PER]
            gathered.append(lax.all_gather(part, "data", axis=0, tiled=False))
        h, prev = x_second, ()
        for (lo, hi), g in zip(CHUNKS, gathered):
            *prev, h = update_forward(lo, hi, h, g, (w_in, w_out, mom_in, mom_out), tuple(prev))
        row_diff = h - y_second.astype(F32)
        loss_rows = jnp.sum(row_diff * row_diff, axis=-1) / (2 * DIM)
        return prev[0], prev[1], prev[2], prev[3], loss_rows, h

    return jax.shard_map(
        local_steps, mesh=mesh,
        in_specs=(P(), P(), P(), P(), rows_spec, rows_spec, rows_spec, rows_spec),
        out_specs=(P(), P(), P(), P(), P("data"), rows_spec), check_vma=False)
```

time: 1840 us -> 688 us (0.37)
  waiting for transfers between devices: 772 us -> 127 us
  Pallas kernels: 0 us -> 538 us
  matrix products: 445 us -> 0 us
  local copies, waits for them, and re-layouts: 317 us -> 7.74 us
  other arithmetic: 276 us -> 2.02 us
    psum x1 -> x0, waiting for transfers between devices: 772 us -> none  [local_steps(): lax.psum((grad_in, grad_out), 'data')]
    pallas_call x0 -> x5, Pallas kernels: none -> 538 us  [the longest x3 245 us: update_forward(): pl.pallas_call(functools.partial(upd_kernel, lo, hi, nalias), grid=(n,),...]
    dot_general x110 -> x0, matrix products: 445 us -> none  [the longest x32 153 us: forward_stack(): h_cur = h_cur + jnp.dot(act_bf, w_out_l, preferred_element_type=jnp.float32)]
    unnamed x293 -> x2, local copies, waits for them, and re-layouts: 314 us -> 0.01 us
    another operation x4 -> x0, other arithmetic: 275 us -> none
    all_gather x0 -> x3, waiting for transfers between devices: none -> 127 us  [local_steps(): gathered.append(lax.all_gather(part, 'data', axis=0, tiled=False))]
  transfers between devices with their start and end apart: 1 -> 3, of which waited for: 1 -> 1; matrix products, arithmetic and copies ran while one was open for 7% -> 1% of each run, Pallas kernels for 0% -> 29%
where the time goes in v1:
time: 688 us
  Pallas kernels  538 us (78%)
  waiting for transfers between devices  127 us (18%)
  between operations  13.8 us (2%)
  local copies, waits for them, and re-layouts  7.74 us (1%)
    pallas_call x3, Pallas kernels, update_forward(): pl.pallas_call(functools.partial(upd_kernel, lo, hi, nalias), grid=(n,),...  245 us
    pallas_call x1, Pallas kernels, backward_scatter(): pl.pallas_call(functools.partial(bwd_kernel, inv), grid=(UNITS + 8,), in_...  228 us
    all_gather x3, waiting for transfers between devices, local_steps(): gathered.append(lax.all_gather(part, 'data', axis=0, tiled=False))  127 us
    pallas_call x1, Pallas kernels, forward_first(): pl.pallas_call(functools.partial(fwd_kernel, tiles), grid=(LAYERS * tiles...  65.1 us
  transfers between devices with their start and end apart: 3, of which 1 were waited for; matrix products, arithmetic and copies ran while one was open for 1% of the time, Pallas kernels for 29%

profile of v1, /device:TPU:0, one launch (start us, length us, event | category | flops | bytes accessed | tf_op | source)
XLA Modules:
  0.0 688.0 jit_solution(10159350690877907919)
XLA Ops:
  7.2 0.0 all-gather.7.cloned.1.call-start
  7.2 65.1 %fwd_first.1 = (bf16[16,512,512]{2,1,0:T(8,128)(2,1)}, f32[512,512]{1,0:T(8,128)}) custom-call(bf16[512,512]{1,0:T(8,128)(2,1)} %x_ref.1, f32[16,512,2048]{2,1,0:T(8,128)} %w1_ref.9, f32[16,2048,512]{2,1,0:T(8,128)} %w2_ref.9), custom_call_target="tpu_custom_call" | custom-call | tf_op jit(solution)/shard_map/fwd_first/pallas_call | solution.py:77
  72.3 227.7 %bwd_scatter.1 = bf16[64,256,128]{2,1,0:T(8,128)(2,1)} custom-call(f32[16,512,2048]{2,1,0:T(8,128)} %w1_ref.9, f32[16,2048,512]{2,1,0:T(8,128)} %w2_ref.9, bf16[16,512,512]{2,1,0:T(8,128)(2,1)} %get-tuple-element.23.hb_ref, f32[512,512]{1,0:T(8,128)} %get-tuple-element.24.hl_ref, bf16[512,512]{1,0:T(8,128)(2,1)} %y_ref.1), custom_call_target="tpu_custom_call" | custom-call | tf_op jit(solution)/shard_map/bwd_scatter/pallas_call | solution.py:231
  299.9 3.1 slice.9
  303.1 0.0 all-gather.7.cloned.1.call-update
  303.1 0.0 all-gather.9.cloned.1.call-start
  303.2 2.5 slice.10
  305.7 0.0 all-gather.9.cloned.1.call-update
  305.7 0.0 all-gather.11.cloned.1.call-start
  305.8 2.1 slice.11
  307.8 0.0 all-gather.11.cloned.1.call-update
  307.9 126.6 %all-gather.7.cloned.1.call-done = bf16[512,256,128]{2,1,0:T(8,128)(2,1)} async-done(((bf16[32,256,128]{2,1,0:T(8,128)(2,1)}), bf16[512,256,128]{2,1,0:T(8,128)(2,1)}) %all-gather.7.cloned.1.call-update) | async-done | bytes 33554448 | tf_op jit(solution)/shard_map/all_gather | solution.py:333
  434.4 121.4 %upd_fwd.3 = (f32[16,512,2048]{2,1,0:T(8,128)}, f32[16,2048,512]{2,1,0:T(8,128)}, f32[16,512,2048]{2,1,0:T(8,128)}, f32[16,2048,512]{2,1,0:T(8,128)}, f32[512,512]{1,0:T(8,128)}) custom-call(bf16[512,512]{1,0:T(8,128)(2,1)} %h_ref.1, bf16[16,32,256,128]{3,2,1,0:T(8,128)(2,1)} %bitcast.3, f32[16,512,2048]{2,1,0:T(8,128)} %w1_ref.9, f32[16,2048,512]{2,1,0:T(8,128)} %w2_ref.9, ...), custom_call_target="tpu_custom_call" | custom-call | flops 17179869184 | bytes 301989888 | tf_op jit(solution)/shard_map/upd_fwd/pallas_call | solution.py:309
  555.8 0.0 all-gather.9.cloned.1.call-done
  555.9 76.7 %upd_fwd.4 = (f32[16,512,2048]{2,1,0:T(8,128)}, f32[16,2048,512]{2,1,0:T(8,128)}, f32[16,512,2048]{2,1,0:T(8,128)}, f32[16,2048,512]{2,1,0:T(8,128)}, f32[512,512]{1,0:T(8,128)}) custom-call(f32[512,512]{1,0:T(8,128)} %get-tuple-element.25.h_ref, ...), custom_call_target="tpu_custom_call", output_to_operand_aliasing={{0}: (6, {}), {1}: (7, {}), {2}: (8, {}), {3}: (9, {})} | custom-call | flops 10737418240 | bytes 188743680 | tf_op jit(solution)/shard_map/upd_fwd/pallas_call | solution.py:309
  632.6 0.0 all-gather.11.cloned.1.call-done
  632.6 0.0 copy-start
  632.6 46.8 %upd_fwd.5 = (f32[16,512,2048]{2,1,0:T(8,128)}, f32[16,2048,512]{2,1,0:T(8,128)}, f32[16,512,2048]{2,1,0:T(8,128)}, f32[16,2048,512]{2,1,0:T(8,128)}, f32[512,512]{1,0:T(8,128)}) custom-call(f32[512,512]{1,0:T(8,128)} %get-tuple-element.30.h_ref, ...), custom_call_target="tpu_custom_call", output_to_operand_aliasing={{0}: (6, {}), {1}: (7, {}), {2}: (8, {}), {3}: (9, {})} | custom-call | flops 6442450944 | bytes 113246208 | tf_op jit(solution)/shard_map/upd_fwd/pallas_call | solution.py:309
  679.4 0.0 copy-done
  679.4 1.4 multiply_reduce_fusion
  680.9 0.6 broadcast_multiply_fusion
Async XLA Ops:
  7.2 427.3 %all-gather.7.cloned.1.call-start = ((), (), s32[]{:S(2)}) async-start(), calls=%async_computation | async-start | bytes 35651584 | tf_op jit(solution)/shard_map/all_gather | solution.py:333
  303.1 252.7 %all-gather.9.cloned.1.call-start = ((), (), s32[]{:S(2)}) async-start(), calls=%async_computation.1 | async-start | bytes 22282240 | tf_op jit(solution)/shard_map/all_gather | solution.py:333
  305.7 326.9 %all-gather.11.cloned.1.call-start = ((), (), s32[]{:S(2)}) async-start(), calls=%async_computation.2 | async-start | bytes 13369344 | tf_op jit(solution)/shard_map/all_gather | solution.py:333
  632.6 46.8 %copy-start = (bf16[512,512]{1,0:T(8,128)(2,1)S(1)}, bf16[512,512]{1,0:T(8,128)(2,1)}, u32[]{:S(2)}) copy-start(bf16[512,512]{1,0:T(8,128)(2,1)} %param.15) | copy-start | bytes 1572868
Sparse Core Ops, SparseCore 0:
  303.2 131.1 all-gather.6
  436.7 89.6 all-gather.8
  528.6 62.3 all-gather.10

commit v2 on v1

--- a/solution.py
+++ b/solution.py
@@ -23,8 +23,12 @@
 HALF = (80, 80, 96)
 HSTART = (0, 80, 160)
 RING = 8
-CHUNKS = ((0, 8), (8, 13), (13, 16))
-VMEM_LIMIT = 60 * 2**20
+ARING = 16
+DEPTH = 18
+CHUNKS = ((0, 6), (6, 11), (11, 14), (14, 16))
+SPANS = tuple(((LAYERS - hi) * PER, (hi - lo) * PER) for lo, hi in CHUNKS)
+SUB = 2
+VMEM_LIMIT = 62 * 2**20
 
 
 def dot(a, b, ca=1, cb=0):
@@ -71,7 +75,7 @@
 
 
 def forward_first(x, w_in, w_out):
-    tiles = 2
+    tiles = 1
     th = HID // tiles
     full = pl.BlockSpec((ROWS, DIM), lambda i: (0, 0))
     return pl.pallas_call(
@@ -94,10 +98,14 @@
 
 
 def bwd_kernel(
-    inv, w1_ref, w2_ref, hb_ref, hl_ref, y_ref, out_ref,
-    e_s, eb_s, ht_s, gst, rb, acc, rv1, rv2, rv3,
-    s0, r0, s1, r1, s2, r2, s3, r3,
+    inv, w1_ref, w2_ref, hb_ref, hl_ref, y_ref, *rest,
 ):
+    full_ref, out_refs, (
+        e_s, eb_s, ht_s, gst, rb, acc, gb, rv1, rv2, rv3, tv3,
+        s0, r0, s1, r1, s2, r2, s3, r3,
+        ts0, tr0, ts1, tr1, ts2, tr2, ts3, tr3, ls,
+    ) = rest[0], rest[1:len(CHUNKS)], rest[len(CHUNKS):]
+    whole = SPANS[0][0]
     i = pl.program_id(0)
     me = lax.axis_index("data")
     core = lax.rem(me, 2)
@@ -130,44 +138,115 @@
 
     def stage_copy(u, k, p):
         bits, peers = geometry(u, k)
-        slot = lax.rem(u, RING)
+        slot, aslot = lax.rem(u, RING), lax.rem(u, ARING)
         hs = pl.ds(HSTART[k], HALF[k])
         if p == 0:
-            src, dst = acc.at[slot, rows_of(k, 1 - bits[0])], rv1.at[slot, hs]
+            src, dst = acc.at[aslot, rows_of(k, 1 - bits[0])], rv1.at[slot, hs]
         elif p == 1:
-            src, dst = acc.at[slot, rows_of(k, bits[0]), cols_of((1 - bits[1]) * 256, 256)], rv2.at[slot, hs]
+            src, dst = acc.at[aslot, rows_of(k, bits[0]), cols_of((1 - bits[1]) * 256, 256)], rv2.at[slot, hs]
         else:
-            src = acc.at[slot, rows_of(k, bits[0]), cols_of(bits[1] * 256 + (1 - bits[2]) * 128, 128)]
+            src = acc.at[aslot, rows_of(k, bits[0]), cols_of(bits[1] * 256 + (1 - bits[2]) * 128, 128)]
             dst = rv3.at[slot, hs]
         ss, rs = ((s1, r1), (s2, r2), (s3, r3))[p]
         return pltpu.make_async_remote_copy(
             src_ref=src, dst_ref=dst, send_sem=ss.at[lax.rem(u, 4), k], recv_sem=rs.at[slot, k],
             device_id=(peers[p],), device_id_type=MESH)
 
+    def gather_copy(u, k, p):
+        bits, peers = geometry(u, k)
+        cols = (pl.ds(0, DIM), cols_of(bits[1] * 256, 256), cols_of(bits[1] * 256 + bits[2] * 128, 128))[p]
+        part = acc.at[lax.rem(u, ARING), rows_of(k, bits[0]), cols]
+        into = tv3.at[lax.rem(u, RING), pl.ds(HSTART[k], HALF[k])] if p == 2 else part
+        ss, rs = ((ts1, tr1), (ts2, tr2), (ts3, tr3))[p]
+        return pltpu.make_async_remote_copy(
+            src_ref=part, dst_ref=into, send_sem=ss.at[lax.rem(u, 4), k], recv_sem=rs.at[lax.rem(u, RING), k],
+            device_id=(peers[p],), device_id_type=MESH)
+
+    def gather_core(u):
+        return pltpu.make_async_remote_copy(
+            src_ref=acc.at[lax.rem(u, ARING)], dst_ref=gb.at[lax.rem(u, RING)],
+            send_sem=ts0.at[lax.rem(u, 4)], recv_sem=tr0.at[lax.rem(u, RING)],
+            device_id=(sib,), device_id_type=MESH)
+
+    def store_copies(u):
+        n, j = u - whole, lax.rem(u, 4)
+        return (pltpu.make_async_copy(acc.at[lax.rem(u, ARING)], full_ref.at[n, core], ls.at[j, 0]),
+                pltpu.make_async_copy(gb.at[lax.rem(u, RING)], full_ref.at[n, 1 - core], ls.at[j, 1]))
+
     def add(a, b):
         return (a.astype(F32) + b.astype(F32)).astype(BF)
 
-    @pl.when(i >= 8)
+    def gathering(lag):
+        return (i >= whole + lag) & (i < UNITS + lag)
+
+    @pl.when(gathering(18))
+    def _():
+        for c in store_copies(i - 18):
+            c.wait()
+
+    @pl.when(gathering(16))
+    def _():
+        gather_core(i - 16).wait()
+        for c in store_copies(i - 16):
+            c.start()
+
+    @pl.when(gathering(14))
+    def _():
+        for k in range(3):
+            gather_copy(i - 14, k, 0).wait()
+        gather_core(i - 14).start()
+
+    @pl.when(gathering(12))
+    def _():
+        for k in range(3):
+            gather_copy(i - 12, k, 1).wait()
+        for k in range(3):
+            gather_copy(i - 12, k, 0).start()
+
+    @pl.when(gathering(10))
+    def _():
+        u = i - 10
+        for k in range(3):
+            gather_copy(u, k, 2).wait()
+        for k in range(3):
+            bits, _ = geometry(u, k)
+            cols = cols_of(bits[1] * 256 + (1 - bits[2]) * 128, 128)
+            acc[lax.rem(u, ARING), rows_of(k, bits[0]), cols] = tv3[lax.rem(u, RING), pl.ds(HSTART[k], HALF[k]), :]
+        for k in range(3):
+            gather_copy(u, k, 1).start()
+
+    @pl.when((i >= 8) & (i < UNITS + 8))
     def _():
         u = i - 8
-        slot = lax.rem(u, RING)
+        slot, aslot = lax.rem(u, RING), lax.rem(u, ARING)
         for k in range(3):
             stage_copy(u, k, 2).wait()
         for k in range(3):
             bits, _ = geometry(u, k)
             hs = pl.ds(HSTART[k], HALF[k])
-            out_ref[0, hs, :] = add(acc[slot, rows_of(k, bits[0]), cols_of(bits[1] * 256 + bits[2] * 128, 128)], rv3[slot, hs, :])
+            idx = (aslot, rows_of(k, bits[0]), cols_of(bits[1] * 256 + bits[2] * 128, 128))
+            done = add(acc[idx], rv3[slot, hs, :])
+
+            @pl.when(u >= whole)
+            def _():
+                acc[idx] = done
+                gather_copy(u, k, 2).start()
+
+            for (first, count), out_ref in zip(SPANS[1:], out_refs):
+                @pl.when((u >= first) & (u < first + count))
+                def _(out_ref=out_ref):
+                    out_ref[0, hs, :] = done
 
     @pl.when((i >= 6) & (i < UNITS + 6))
     def _():
         u = i - 6
-        slot = lax.rem(u, RING)
+        slot, aslot = lax.rem(u, RING), lax.rem(u, ARING)
         for k in range(3):
             stage_copy(u, k, 1).wait()
         for k in range(3):
             bits, _ = geometry(u, k)
             hs = pl.ds(HSTART[k], HALF[k])
-            idx = (slot, rows_of(k, bits[0]), cols_of(bits[1] * 256, 256))
+            idx = (aslot, rows_of(k, bits[0]), cols_of(bits[1] * 256, 256))
             acc[idx] = add(acc[idx], rv2[slot, hs, :])
         for k in range(3):
             stage_copy(u, k, 2).start()
@@ -175,13 +254,13 @@
     @pl.when((i >= 4) & (i < UNITS + 4))
     def _():
         u = i - 4
-        slot = lax.rem(u, RING)
+        slot, aslot = lax.rem(u, RING), lax.rem(u, ARING)
         for k in range(3):
             stage_copy(u, k, 0).wait()
         for k in range(3):
             bits, _ = geometry(u, k)
             hs = pl.ds(HSTART[k], HALF[k])
-            idx = (slot, rows_of(k, bits[0]), pl.ds(0, DIM))
+            idx = (aslot, rows_of(k, bits[0]), pl.ds(0, DIM))
             acc[idx] = add(acc[idx], rv1[slot, hs, :])
         for k in range(3):
             stage_copy(u, k, 1).start()
@@ -189,9 +268,9 @@
     @pl.when((i >= 2) & (i < UNITS + 2))
     def _():
         u = i - 2
-        slot = lax.rem(u, RING)
+        slot, aslot = lax.rem(u, RING), lax.rem(u, ARING)
         core_copy(u).wait()
-        acc[slot] = add(gst[lax.rem(u, 4), core], rb[slot])
+        acc[aslot] = add(gst[lax.rem(u, 4), core], rb[slot])
         for k in range(3):
             stage_copy(u, k, 0).start()
 
@@ -220,6 +299,10 @@
         core_copy(i).start()
 
 
+def shard_map_of(first, count, i):
+    return jnp.clip(i - 8 - first, 0, count - 1), 0, 0
+
+
 def backward_scatter(w_in, w_out, hs, hl, y, inv):
     last = UNITS - 1
 
@@ -230,21 +313,24 @@
     dma = pltpu.SemaphoreType.DMA
     return pl.pallas_call(
         functools.partial(bwd_kernel, inv),
-        grid=(UNITS + 8,),
+        grid=(UNITS + DEPTH,),
         in_specs=[
             pl.BlockSpec((1, DIM, TILE), lambda i: (layer(i), 0, jnp.minimum(i, last) % PER)),
             pl.BlockSpec((1, TILE, DIM), lambda i: (layer(i), jnp.minimum(i, last) % PER, 0)),
             pl.BlockSpec((1, ROWS, DIM), lambda i: (layer(i), 0, 0)),
             full, full,
         ],
-        out_specs=pl.BlockSpec((1, 256, 128), lambda i: (jnp.maximum(i - 8, 0), 0, 0)),
-        out_shape=jax.ShapeDtypeStruct((UNITS, 256, 128), BF),
+        out_specs=[pl.BlockSpec(memory_space=pl.ANY)] + [
+            pl.BlockSpec((1, 256, 128), functools.partial(shard_map_of, f, n)) for f, n in SPANS[1:]],
+        out_shape=[jax.ShapeDtypeStruct((SPANS[0][1], 2, 512, 512), BF)] + [
+            jax.ShapeDtypeStruct((n, 256, 128), BF) for _, n in SPANS[1:]],
         scratch_shapes=[
             pltpu.VMEM((ROWS, DIM), F32), pltpu.VMEM((ROWS, DIM), BF), pltpu.VMEM((DIM, ROWS), BF),
-            pltpu.VMEM((4, 2, 512, 512), BF), pltpu.VMEM((RING, 512, 512), BF), pltpu.VMEM((RING, 512, 512), BF),
+            pltpu.VMEM((4, 2, 512, 512), BF), pltpu.VMEM((RING, 512, 512), BF), pltpu.VMEM((ARING, 512, 512), BF),
+            pltpu.VMEM((RING, 512, 512), BF),
             pltpu.VMEM((RING, 256, 512), BF), pltpu.VMEM((RING, 256, 256), BF), pltpu.VMEM((RING, 256, 128), BF),
-            dma((4,)), dma((RING,)), dma((4, 3)), dma((RING, 3)), dma((4, 3)), dma((RING, 3)), dma((4, 3)), dma((RING, 3)),
-        ],
+            pltpu.VMEM((RING, 256, 128), BF),
+        ] + [dma(n) for n in ((4,), (RING,)) + ((4, 3), (RING, 3)) * 3] * 2 + [dma((4, 2))],
         compiler_params=pltpu.CompilerParams(
             vmem_limit_bytes=VMEM_LIMIT, collective_id=0, has_side_effects=True),
         name="bwd_scatter",
@@ -252,57 +338,82 @@
 
 
 def upd_kernel(lo, hi, nalias, h_ref, g_ref, w1_ref, w2_ref, m1_ref, m2_ref, *rest):
-    w1o, w2o, m1o, m2o, ho_ref, h_s, hb_s = rest[nalias:]
+    w1o, w2o, m1o, m2o, ho_ref, h_s, hb_s, wb1, wb2 = rest[nalias:]
     i = pl.program_id(0)
-    layer = lo + i // PER
-    rot = lax.rem((LAYERS - 1 - layer) * PER + lax.rem(i, PER), 3)
+    steps = PER // SUB
+    layer = lo + i // steps
 
     @pl.when(i == 0)
     def _():
         h_s[...] = h_ref[...].astype(F32)
 
-    @pl.when(lax.rem(i, PER) == 0)
+    @pl.when(lax.rem(i, steps) == 0)
     def _():
         hb_s[...] = h_s[...].astype(BF)
 
-    def chip(q, _):
+    def chip(q, t, rot):
         for k in range(3):
             bits = []
             for p in range(3):
                 a = lax.rem(rot + k + p, 3)
                 stride = lax.div(a * a + a + 2, 2)
                 bits.append(lax.rem(lax.div(q, stride), 2))
-            rows = pl.ds(pl.multiple_of(START[k] + bits[0] * HALF[k], 16), HALF[k])
-            cols = pl.ds(pl.multiple_of(bits[1] * 256 + bits[2] * 128, 128), 128)
-            for c, (w, m, wo, mo) in enumerate(((w1_ref, m1_ref, w1o, m1o), (w2_ref, m2_ref, w2o, m2o))):
-                g = g_ref[2 * q + c, 0, pl.ds(HSTART[k], HALF[k]), :].astype(F32)
+            row = START[k] + bits[0] * HALF[k]
+            col = bits[1] * 256 + bits[2] * 128
+            for c, (w, m, wo, mo, wb) in enumerate(((w1_ref, m1_ref, w1o, m1o, wb1), (w2_ref, m2_ref, w2o, m2o, wb2))):
+                rows = pl.ds(pl.multiple_of(row + c * t * TILE, 16), HALF[k])
+                cols = pl.ds(pl.multiple_of(col + (1 - c) * t * TILE, 128), 128)
+                g = g_ref[2 * q + c, t, pl.ds(HSTART[k], HALF[k]), :].astype(F32)
                 mn = MU * m[0, rows, cols] + g
+                wn = w[0, rows, cols] - STEP * mn
                 mo[0, rows, cols] = mn
-                wo[0, rows, cols] = w[0, rows, cols] - STEP * mn
-        return 0
-
-    lax.fori_loop(0, 8, chip, 0)
-    z = dot(hb_s[...], w1o[0].astype(BF))
-    h_s[...] += dot(gelu(z).astype(BF), w2o[0].astype(BF))
-
-    @pl.when(i == (hi - lo) * PER - 1)
+                wo[0, rows, cols] = wn
+                wb[rows, cols] = wn.astype(BF)
+
+    for t in range(SUB):
+        rot = lax.rem((LAYERS - 1 - layer) * PER + lax.rem(i, steps) * SUB + t, 3)
+
+        def body(q, _, t=t, rot=rot):
+            chip(q, t, rot)
+            return 0
+
+        def rows_body(r, _, t=t):
+            for c, (w, m, wo, mo, wb) in enumerate(((w1_ref, m1_ref, w1o, m1o, wb1), (w2_ref, m2_ref, w2o, m2o, wb2))):
+                rows = pl.ds(pl.multiple_of(r * 32 + c * t * TILE, 32), 32)
+                cols = pl.ds((1 - c) * t * TILE, TILE)
+                mn = MU * m[0, rows, cols] + g_ref[t, c, pl.ds(pl.multiple_of(r * 32, 32), 32), :].astype(F32)
+                wn = w[0, rows, cols] - STEP * mn
+                mo[0, rows, cols] = mn
+                wo[0, rows, cols] = wn
+                wb[rows, cols] = wn.astype(BF)
+            return 0
+
+        if lo == 0:
+            lax.fori_loop(0, 16, rows_body, 0, unroll=2)
+        else:
+            lax.fori_loop(0, 8, body, 0, unroll=2)
+    z = dot(hb_s[...], wb1[...])
+    h_s[...] += dot(gelu(z).astype(BF), wb2[...])
+
+    @pl.when(i == (hi - lo) * steps - 1)
     def _():
         ho_ref[...] = h_s[...]
 
 
 def update_forward(lo, hi, h, g, weights, prev):
-    n = (hi - lo) * PER
-
-    def in_map(i):
-        return (lo + i // PER, 0, i % PER)
-
-    def out_map(i):
-        return (lo + i // PER, i % PER, 0)
-
-    b1 = pl.BlockSpec((1, DIM, TILE), in_map)
-    b2 = pl.BlockSpec((1, TILE, DIM), out_map)
+    steps = PER // SUB
+    n = (hi - lo) * steps
+    wide = SUB * TILE
+    b1 = pl.BlockSpec((1, DIM, wide), lambda i: (lo + i // steps, 0, i % steps))
+    b2 = pl.BlockSpec((1, wide, DIM), lambda i: (lo + i // steps, i % steps, 0))
     full = pl.BlockSpec((ROWS, DIM), lambda i: (0, 0))
-    gspec = pl.BlockSpec((16, 1, 256, 128), lambda i: (0, (hi - lo - 1 - i // PER) * PER + i % PER, 0, 0))
+    def order(i):
+        return (hi - lo - 1 - i // steps) * steps + i % steps
+
+    if lo == 0:
+        gspec = pl.BlockSpec((SUB, 2, 512, 512), lambda i: (order(i), 0, 0, 0))
+    else:
+        gspec = pl.BlockSpec((16, SUB, 256, 128), lambda i: (0, order(i), 0, 0))
     nalias = len(prev)
     s1 = jax.ShapeDtypeStruct((LAYERS, DIM, HID), F32)
     s2 = jax.ShapeDtypeStruct((LAYERS, HID, DIM), F32)
@@ -313,9 +424,11 @@
         out_specs=[b1, b2, b1, b2, full],
         out_shape=[s1, s2, s1, s2, jax.ShapeDtypeStruct((ROWS, DIM), F32)],
         input_output_aliases={6 + a: a for a in range(nalias)},
-        scratch_shapes=[pltpu.VMEM((ROWS, DIM), F32), pltpu.VMEM((ROWS, DIM), BF)],
+        scratch_shapes=[
+            pltpu.VMEM((ROWS, DIM), F32), pltpu.VMEM((ROWS, DIM), BF),
+            pltpu.VMEM((DIM, wide), BF), pltpu.VMEM((wide, DIM), BF)],
         compiler_params=pltpu.CompilerParams(vmem_limit_bytes=VMEM_LIMIT),
-        cost_estimate=pl.CostEstimate(flops=n * 4 * 512**3, bytes_accessed=n * 9 * 2**20, transcendentals=0),
+        cost_estimate=pl.CostEstimate(flops=n * SUB * 4 * 512**3, bytes_accessed=n * SUB * 9 * 2**20, transcendentals=0),
         name="upd_fwd",
     )(h, g, *weights, *prev)
 
@@ -326,11 +439,8 @@
 
     def local_steps(w_in, w_out, mom_in, mom_out, x_first, y_first, x_second, y_second):
         hs, hl = forward_first(x_first, w_in, w_out)
-        shards = backward_scatter(w_in, w_out, hs, hl, y_first, 1.0 / (ROWS * groups * DIM))
-        gathered = []
-        for lo, hi in CHUNKS:
-            part = shards[(LAYERS - hi) * PER:(LAYERS - lo) * PER]
-            gathered.append(lax.all_gather(part, "data", axis=0, tiled=False))
+        first, *shards = backward_scatter(w_in, w_out, hs, hl, y_first, 1.0 / (ROWS * groups * DIM))
+        gathered = [first] + [lax.all_gather(part, "data", axis=0, tiled=False) for part in shards]
         h, prev = x_second, ()
         for (lo, hi), g in zip(CHUNKS, gathered):
             *prev, h = update_forward(lo, hi, h, g, (w_in, w_out, mom_in, mom_out), tuple(prev))

time: 688 us -> 613 us (0.89)
  waiting for transfers between devices: 127 us -> 17.3 us
  Pallas kernels: 538 us -> 579 us
  local copies, waits for them, and re-layouts: 7.74 us -> 0.01 us
    all_gather x3, waiting for transfers between devices: 127 us -> 16.1 us  [local_steps(): lax.all_gather(part, 'data', axis=0, tiled=False)]
    pallas_call x1, Pallas kernels: 228 us -> 308 us  [backward_scatter(): pl.pallas_call(functools.partial(bwd_kernel, inv), grid=(UNITS + DEPTH,),...]
    pallas_call x3 -> x4, Pallas kernels: 245 us -> 216 us  [update_forward(): pl.pallas_call(functools.partial(upd_kernel, lo, hi, nalias), grid=(n,),...]
    pallas_call x1, Pallas kernels: 65.1 us -> 55.2 us  [forward_first(): pl.pallas_call(functools.partial(fwd_kernel, tiles), grid=(LAYERS * tiles...]
    slice x3 -> x0, local copies, waits for them, and re-layouts: 7.73 us -> none  [local_steps(): part = shards[(LAYERS - hi) * PER:(LAYERS - lo) * PER]]
  transfers between devices with their start and end apart: 3 -> 3, of which waited for: 1 -> 2; matrix products, arithmetic and copies ran while one was open for 1% -> 0% of each run, Pallas kernels for 29% -> 31%
where the time goes in v2:
time: 613 us; the launch traced here: 612 us
  Pallas kernels  579 us (94%)
  waiting for transfers between devices  17.3 us (3%)
  between operations  13.8 us (2%)
    pallas_call x1, Pallas kernels, backward_scatter(): pl.pallas_call(functools.partial(bwd_kernel, inv), grid=(UNITS + DEPTH,),...  308 us
    pallas_call x4, Pallas kernels, update_forward(): pl.pallas_call(functools.partial(upd_kernel, lo, hi, nalias), grid=(n,),...  216 us
    pallas_call x1, Pallas kernels, forward_first(): pl.pallas_call(functools.partial(fwd_kernel, tiles), grid=(LAYERS * tiles...  55.2 us
    all_gather x3, waiting for transfers between devices, local_steps(): lax.all_gather(part, 'data', axis=0, tiled=False)  16.1 us
  transfers between devices with their start and end apart: 3, of which 2 were waited for; matrix products, arithmetic and copies ran while one was open for 0% of the time, Pallas kernels for 31%

profile of v2, /device:TPU:0, one launch (start us, length us, event | category | flops | bytes accessed | tf_op | source)
XLA Modules:
  0.0 612.4 jit_solution(16761045808253362801)
XLA Ops:
  7.2 0.0 all-gather.7.cloned.1.call-start
  7.2 55.2 %fwd_first.1 = (bf16[16,512,512]{2,1,0:T(8,128)(2,1)}, f32[512,512]{1,0:T(8,128)}) custom-call(bf16[512,512]{1,0:T(8,128)(2,1)} %x_ref.1, f32[16,512,2048]{2,1,0:T(8,128)} %w1_ref.11, f32[16,2048,512]{2,1,0:T(8,128)} %w2_ref.11), custom_call_target="tpu_custom_call" | custom-call | tf_op jit(solution)/shard_map/fwd_first/pallas_call | solution.py:81
  62.4 308.1 %bwd_scatter.1 = (bf16[24,2,512,512]{3,2,1,0:T(8,128)(2,1)}, bf16[20,256,128]{2,1,0:T(8,128)(2,1)}, bf16[12,256,128]{2,1,0:T(8,128)(2,1)}, bf16[8,256,128]{2,1,0:T(8,128)(2,1)}) custom-call(f32[16,512,2048]{2,1,0:T(8,128)} %w1_ref.11, f32[16,2048,512]{2,1,0:T(8,128)} %w2_ref.11, bf16[16,512,512]{2,1,0:T(8,128)(2,1)} %get-tuple-element.32.hb_ref, ...), custom_call_target="tpu_custom_call" | custom-call | tf_op jit(solution)/shard_map/bwd_scatter/pallas_call | solution.py:314
  370.6 0.0 all-gather.7.cloned.1.call-update
  370.6 0.0 all-gather.9.cloned.1.call-start
  370.7 0.7 all-gather.9.cloned.1.call-update
  371.4 0.2 all-gather.11.cloned.1.call-start
  371.6 0.5 all-gather.11.cloned.1.call-update
  372.1 75.9 %upd_fwd.4 = (f32[16,512,2048]{2,1,0:T(8,128)}, f32[16,2048,512]{2,1,0:T(8,128)}, f32[16,512,2048]{2,1,0:T(8,128)}, f32[16,2048,512]{2,1,0:T(8,128)}, f32[512,512]{1,0:T(8,128)}) custom-call(bf16[512,512]{1,0:T(8,128)(2,1)} %h_ref.1, bf16[24,2,512,512]{3,2,1,0:T(8,128)(2,1)} %get-tuple-element.34.g_ref, f32[16,512,2048]{2,1,0:T(8,128)} %w1_ref.11, ...), custom_call_target="tpu_custom_call" | custom-call | flops 12884901888 | bytes 226492416 | tf_op jit(solution)/shard_map/upd_fwd/pallas_call | solution.py:420
  448.0 11.6 %all-gather.7.cloned.1.call-done = bf16[320,256,128]{2,1,0:T(8,128)(2,1)} async-done(((bf16[20,256,128]{2,1,0:T(8,128)(2,1)}), bf16[320,256,128]{2,1,0:T(8,128)(2,1)}) %all-gather.7.cloned.1.call-update) | async-done | bytes 20971536 | tf_op jit(solution)/shard_map/all_gather | solution.py:443
  459.7 68.9 %upd_fwd.5 = (f32[16,512,2048]{2,1,0:T(8,128)}, f32[16,2048,512]{2,1,0:T(8,128)}, f32[16,512,2048]{2,1,0:T(8,128)}, f32[16,2048,512]{2,1,0:T(8,128)}, f32[512,512]{1,0:T(8,128)}) custom-call(f32[512,512]{1,0:T(8,128)} %get-tuple-element.35.h_ref, ...), custom_call_target="tpu_custom_call", output_to_operand_aliasing={{0}: (6, {}), {1}: (7, {}), {2}: (8, {}), {3}: (9, {})} | custom-call | flops 10737418240 | bytes 188743680 | tf_op jit(solution)/shard_map/upd_fwd/pallas_call | solution.py:420
  528.6 0.0 all-gather.9.cloned.1.call-done
  528.6 42.1 %upd_fwd.6 = (f32[16,512,2048]{2,1,0:T(8,128)}, f32[16,2048,512]{2,1,0:T(8,128)}, f32[16,512,2048]{2,1,0:T(8,128)}, f32[16,2048,512]{2,1,0:T(8,128)}, f32[512,512]{1,0:T(8,128)}) custom-call(f32[512,512]{1,0:T(8,128)} %get-tuple-element.41.h_ref, ...), custom_call_target="tpu_custom_call", output_to_operand_aliasing={{0}: (6, {}), {1}: (7, {}), {2}: (8, {}), {3}: (9, {})} | custom-call | flops 6442450944 | bytes 113246208 | tf_op jit(solution)/shard_map/upd_fwd/pallas_call | solution.py:420
  570.7 4.4 all-gather.11.cloned.1.call-done
  575.2 0.0 copy-start
  575.2 28.7 %upd_fwd.7 = (f32[16,512,2048]{2,1,0:T(8,128)}, f32[16,2048,512]{2,1,0:T(8,128)}, f32[16,512,2048]{2,1,0:T(8,128)}, f32[16,2048,512]{2,1,0:T(8,128)}, f32[512,512]{1,0:T(8,128)}) custom-call(f32[512,512]{1,0:T(8,128)} %get-tuple-element.47.h_ref, ...), custom_call_target="tpu_custom_call", output_to_operand_aliasing={{0}: (6, {}), {1}: (7, {}), {2}: (8, {}), {3}: (9, {})} | custom-call | flops 4294967296 | bytes 75497472 | tf_op jit(solution)/shard_map/upd_fwd/pallas_call | solution.py:420
  603.8 0.0 copy-done
  603.9 1.4 multiply_reduce_fusion
  605.3 0.6 broadcast_multiply_fusion
Async XLA Ops:
  7.2 452.5 %all-gather.7.cloned.1.call-start = ((), (), s32[]{:S(2)}) async-start(), calls=%async_computation | async-start | bytes 22282240 | tf_op jit(solution)/shard_map/all_gather | solution.py:443
  370.6 158.0 %all-gather.9.cloned.1.call-start = ((), (), s32[]{:S(2)}) async-start(), calls=%async_computation.1 | async-start | bytes 13369344 | tf_op jit(solution)/shard_map/all_gather | solution.py:443
  371.4 203.8 %all-gather.11.cloned.1.call-start = ((), (), s32[]{:S(2)}) async-start(), calls=%async_computation.2 | async-start | bytes 8912896 | tf_op jit(solution)/shard_map/all_gather | solution.py:443
  575.2 28.7 %copy-start = (bf16[512,512]{1,0:T(8,128)(2,1)S(1)}, bf16[512,512]{1,0:T(8,128)(2,1)}, u32[]{:S(2)}) copy-start(bf16[512,512]{1,0:T(8,128)(2,1)} %param.15) | copy-start | bytes 1572868
Sparse Core Ops, SparseCore 0:
  370.7 88.8 all-gather.6
  461.9 62.2 all-gather.8
  526.5 48.6 all-gather.10

commit v3 on v2

--- a/solution.py
+++ b/solution.py
@@ -25,9 +25,10 @@
 RING = 8
 ARING = 16
 DEPTH = 18
-CHUNKS = ((0, 6), (6, 11), (11, 14), (14, 16))
+CHUNKS = ((0, 7), (7, 12), (12, 15), (15, 16))
+AHEAD = 4
+SLOTS = 8
 SPANS = tuple(((LAYERS - hi) * PER, (hi - lo) * PER) for lo, hi in CHUNKS)
-SUB = 2
 VMEM_LIMIT = 62 * 2**20
 
 
@@ -53,45 +54,60 @@
     return bit, me + (1 - 2 * bit) * stride
 
 
-def fwd_kernel(tiles, x_ref, w1_ref, w2_ref, hs_ref, hl_ref, h_s, hb_s):
+def fwd_kernel(x_ref, w1_hbm, w2_hbm, hs_ref, hl_ref, h_s, hb_s, w1_s, w2_s, sem):
     i = pl.program_id(0)
-    j = lax.rem(i, tiles)
+
+    def load(layer, c):
+        slot = lax.rem(layer, 3)
+        src, dst = ((w1_hbm, w1_s), (w2_hbm, w2_s))[c]
+        return pltpu.make_async_copy(src.at[layer], dst.at[slot], sem.at[slot, c])
 
     @pl.when(i == 0)
     def _():
+        for c in range(2):
+            load(0, c).start()
         h_s[...] = x_ref[...].astype(F32)
 
-    @pl.when(j == 0)
-    def _():
-        hb_s[...] = h_s[...].astype(BF)
-        hs_ref[0] = hb_s[...]
-
-    z = dot(hb_s[...], w1_ref[0].astype(BF))
-    h_s[...] += dot(gelu(z).astype(BF), w2_ref[0].astype(BF))
-
-    @pl.when(i == LAYERS * tiles - 1)
+    hb_s[...] = h_s[...].astype(BF)
+    hs_ref[0] = hb_s[...]
+    slot = lax.rem(i, 3)
+    load(i, 0).wait()
+
+    @pl.when(i == 0)
+    def _():
+        for c in range(2):
+            load(1, c).start()
+
+    @pl.when(i + 2 < LAYERS)
+    def _():
+        for c in range(2):
+            load(i + 2, c).start()
+
+    z = dot(hb_s[...], w1_s[slot].astype(BF))
+    load(i, 1).wait()
+    h_s[...] += dot(gelu(z).astype(BF), w2_s[slot].astype(BF))
+
+    @pl.when(i == LAYERS - 1)
     def _():
         hl_ref[...] = h_s[...]
 
 
 def forward_first(x, w_in, w_out):
-    tiles = 1
-    th = HID // tiles
     full = pl.BlockSpec((ROWS, DIM), lambda i: (0, 0))
+    hbm = pl.BlockSpec(memory_space=pl.ANY)
     return pl.pallas_call(
-        functools.partial(fwd_kernel, tiles),
-        grid=(LAYERS * tiles,),
-        in_specs=[
-            full,
-            pl.BlockSpec((1, DIM, th), lambda i: (i // tiles, 0, i % tiles)),
-            pl.BlockSpec((1, th, DIM), lambda i: (i // tiles, i % tiles, 0)),
-        ],
-        out_specs=[pl.BlockSpec((1, ROWS, DIM), lambda i: (i // tiles, 0, 0)), full],
+        fwd_kernel,
+        grid=(LAYERS,),
+        in_specs=[full, hbm, hbm],
+        out_specs=[pl.BlockSpec((1, ROWS, DIM), lambda i: (i, 0, 0)), full],
         out_shape=[
             jax.ShapeDtypeStruct((LAYERS, ROWS, DIM), BF),
             jax.ShapeDtypeStruct((ROWS, DIM), F32),
         ],
-        scratch_shapes=[pltpu.VMEM((ROWS, DIM), F32), pltpu.VMEM((ROWS, DIM), BF)],
+        scratch_shapes=[
+            pltpu.VMEM((ROWS, DIM), F32), pltpu.VMEM((ROWS, DIM), BF),
+            pltpu.VMEM((3, DIM, HID), F32), pltpu.VMEM((3, HID, DIM), F32),
+            pltpu.SemaphoreType.DMA((3, 2))],
         compiler_params=pltpu.CompilerParams(vmem_limit_bytes=VMEM_LIMIT),
         name="fwd_first",
     )(x, w_in, w_out)
@@ -337,98 +353,121 @@
     )(w_in, w_out, hs, hl, y)
 
 
-def upd_kernel(lo, hi, nalias, h_ref, g_ref, w1_ref, w2_ref, m1_ref, m2_ref, *rest):
-    w1o, w2o, m1o, m2o, ho_ref, h_s, hb_s, wb1, wb2 = rest[nalias:]
+def upd_kernel(lo, hi, nalias, h_ref, g_hbm, *rest):
+    ins, rest = rest[:4], rest[4 + nalias:]
+    outs, ho_ref, (h_s, hb_s, wb1, wb2, sums, gbuf), bufs, (isem, osem) = (
+        rest[:4], rest[4], rest[5:11], rest[11:15], rest[15:])
     i = pl.program_id(0)
-    steps = PER // SUB
-    layer = lo + i // steps
+    n = (hi - lo) * PER
+
+    def window(ref, u, c):
+        tile = pl.ds(pl.multiple_of(lax.rem(u, PER) * TILE, TILE), TILE)
+        layer = lo + lax.div(u, PER)
+        return ref.at[layer, tile, :] if c else ref.at[layer, :, tile]
+
+    def place_of(u):
+        return (hi - lo - 1 - lax.div(u, PER)) * PER + lax.rem(u, PER)
+
+    def loads(u):
+        slot = lax.rem(u, SLOTS)
+        src = g_hbm.at[place_of(u)] if lo == 0 else g_hbm.at[:, place_of(u)]
+        return [pltpu.make_async_copy(window(r, u, a % 2), bufs[a].at[slot], isem.at[slot, a])
+                for a, r in enumerate(ins)] + [pltpu.make_async_copy(src, gbuf.at[slot], isem.at[slot, 4])]
+
+    def stores(u):
+        slot = lax.rem(u, SLOTS)
+        return [pltpu.make_async_copy(bufs[a].at[slot], window(r, u, a % 2), osem.at[slot, a])
+                for a, r in enumerate(outs)]
 
     @pl.when(i == 0)
     def _():
+        for u in range(AHEAD):
+            for c in loads(u):
+                c.start()
         h_s[...] = h_ref[...].astype(F32)
 
-    @pl.when(lax.rem(i, steps) == 0)
+    @pl.when(i >= AHEAD)
+    def _():
+        for c in stores(i - AHEAD):
+            c.wait()
+
+    @pl.when(i + AHEAD < n)
+    def _():
+        for c in loads(i + AHEAD):
+            c.start()
+
+    @pl.when(lax.rem(i, PER) == 0)
     def _():
         hb_s[...] = h_s[...].astype(BF)
 
-    def chip(q, t, rot):
-        for k in range(3):
-            bits = []
-            for p in range(3):
-                a = lax.rem(rot + k + p, 3)
-                stride = lax.div(a * a + a + 2, 2)
-                bits.append(lax.rem(lax.div(q, stride), 2))
-            row = START[k] + bits[0] * HALF[k]
-            col = bits[1] * 256 + bits[2] * 128
-            for c, (w, m, wo, mo, wb) in enumerate(((w1_ref, m1_ref, w1o, m1o, wb1), (w2_ref, m2_ref, w2o, m2o, wb2))):
-                rows = pl.ds(pl.multiple_of(row + c * t * TILE, 16), HALF[k])
-                cols = pl.ds(pl.multiple_of(col + (1 - c) * t * TILE, 128), 128)
-                g = g_ref[2 * q + c, t, pl.ds(HSTART[k], HALF[k]), :].astype(F32)
-                mn = MU * m[0, rows, cols] + g
-                wn = w[0, rows, cols] - STEP * mn
-                mo[0, rows, cols] = mn
-                wo[0, rows, cols] = wn
-                wb[rows, cols] = wn.astype(BF)
-
-    for t in range(SUB):
-        rot = lax.rem((LAYERS - 1 - layer) * PER + lax.rem(i, steps) * SUB + t, 3)
-
-        def body(q, _, t=t, rot=rot):
-            chip(q, t, rot)
-            return 0
-
-        def rows_body(r, _, t=t):
-            for c, (w, m, wo, mo, wb) in enumerate(((w1_ref, m1_ref, w1o, m1o, wb1), (w2_ref, m2_ref, w2o, m2o, wb2))):
-                rows = pl.ds(pl.multiple_of(r * 32 + c * t * TILE, 32), 32)
-                cols = pl.ds((1 - c) * t * TILE, TILE)
-                mn = MU * m[0, rows, cols] + g_ref[t, c, pl.ds(pl.multiple_of(r * 32, 32), 32), :].astype(F32)
-                wn = w[0, rows, cols] - STEP * mn
-                mo[0, rows, cols] = mn
-                wo[0, rows, cols] = wn
-                wb[rows, cols] = wn.astype(BF)
-            return 0
-
-        if lo == 0:
-            lax.fori_loop(0, 16, rows_body, 0, unroll=2)
-        else:
-            lax.fori_loop(0, 8, body, 0, unroll=2)
+    slot = lax.rem(i, SLOTS)
+    for c in loads(i):
+        c.wait()
+
+    if lo:
+        rot = lax.rem((LAYERS - hi) * PER + place_of(i), 3)
+
+        @pl.loop(0, 8)
+        def _(q):
+            for k in range(3):
+                bits = []
+                for p in range(3):
+                    a = lax.rem(rot + k + p, 3)
+                    stride = lax.div(a * a + a + 2, 2)
+                    bits.append(lax.rem(lax.div(q, stride), 2))
+                rows = pl.ds(pl.multiple_of(START[k] + bits[0] * HALF[k], 16), HALF[k])
+                cols = pl.ds(pl.multiple_of(bits[1] * 256 + bits[2] * 128, 128), 128)
+                for c in range(2):
+                    sums[c, rows, cols] = gbuf[slot, 2 * q + c, pl.ds(HSTART[k], HALF[k]), :]
+
+    @pl.loop(0, 16)
+    def _(r):
+        rows = pl.ds(pl.multiple_of(r * 32, 32), 32)
+        for c, wb in enumerate((wb1, wb2)):
+            w, m = bufs[c], bufs[2 + c]
+            g = sums[c, rows, :] if lo else gbuf[slot, c, rows, :]
+            mn = MU * m[slot, rows, :] + g.astype(F32)
+            wn = w[slot, rows, :] - STEP * mn
+            m[slot, rows, :] = mn
+            w[slot, rows, :] = wn
+            wb[rows, :] = wn.astype(BF)
+
+    for c in stores(i):
+        c.start()
     z = dot(hb_s[...], wb1[...])
     h_s[...] += dot(gelu(z).astype(BF), wb2[...])
 
-    @pl.when(i == (hi - lo) * steps - 1)
+    @pl.when(i == n - 1)
     def _():
         ho_ref[...] = h_s[...]
+        for u in range(n - AHEAD, n):
+            for c in stores(u):
+                c.wait()
 
 
 def update_forward(lo, hi, h, g, weights, prev):
-    steps = PER // SUB
-    n = (hi - lo) * steps
-    wide = SUB * TILE
-    b1 = pl.BlockSpec((1, DIM, wide), lambda i: (lo + i // steps, 0, i % steps))
-    b2 = pl.BlockSpec((1, wide, DIM), lambda i: (lo + i // steps, i % steps, 0))
+    n = (hi - lo) * PER
     full = pl.BlockSpec((ROWS, DIM), lambda i: (0, 0))
-    def order(i):
-        return (hi - lo - 1 - i // steps) * steps + i % steps
-
-    if lo == 0:
-        gspec = pl.BlockSpec((SUB, 2, 512, 512), lambda i: (order(i), 0, 0, 0))
-    else:
-        gspec = pl.BlockSpec((16, SUB, 256, 128), lambda i: (0, order(i), 0, 0))
+    hbm = pl.BlockSpec(memory_space=pl.ANY)
     nalias = len(prev)
     s1 = jax.ShapeDtypeStruct((LAYERS, DIM, HID), F32)
     s2 = jax.ShapeDtypeStruct((LAYERS, HID, DIM), F32)
+    gshape = (2, 512, 512) if lo == 0 else (16, 256, 128)
+    tile = (TILE, DIM)
     return pl.pallas_call(
         functools.partial(upd_kernel, lo, hi, nalias),
         grid=(n,),
-        in_specs=[full, gspec, b1, b2, b1, b2] + [pl.BlockSpec(memory_space=pl.ANY)] * nalias,
-        out_specs=[b1, b2, b1, b2, full],
+        in_specs=[full] + [hbm] * (5 + nalias),
+        out_specs=[hbm] * 4 + [full],
         out_shape=[s1, s2, s1, s2, jax.ShapeDtypeStruct((ROWS, DIM), F32)],
         input_output_aliases={6 + a: a for a in range(nalias)},
         scratch_shapes=[
-            pltpu.VMEM((ROWS, DIM), F32), pltpu.VMEM((ROWS, DIM), BF),
-            pltpu.VMEM((DIM, wide), BF), pltpu.VMEM((wide, DIM), BF)],
+            pltpu.VMEM((ROWS, DIM), F32), pltpu.VMEM((ROWS, DIM), BF), pltpu.VMEM(tile, BF), pltpu.VMEM(tile, BF),
+            pltpu.VMEM((2,) + tile, BF), pltpu.VMEM((SLOTS,) + gshape, BF),
+        ] + [pltpu.VMEM((SLOTS,) + tile, F32)] * 4 + [
+            pltpu.SemaphoreType.DMA((SLOTS, 5)), pltpu.SemaphoreType.DMA((SLOTS, 4))],
         compiler_params=pltpu.CompilerParams(vmem_limit_bytes=VMEM_LIMIT),
-        cost_estimate=pl.CostEstimate(flops=n * SUB * 4 * 512**3, bytes_accessed=n * SUB * 9 * 2**20, transcendentals=0),
+        cost_estimate=pl.CostEstimate(flops=n * 4 * 512**3, bytes_accessed=n * 9 * 2**20, transcendentals=0),
         name="upd_fwd",
     )(h, g, *weights, *prev)
 

time: 613 us -> 596 us (0.972)
  waiting for transfers between devices: 17.3 us -> 4.04 us
    all_gather x3, waiting for transfers between devices: 16.1 us -> 2.65 us  [local_steps(): lax.all_gather(part, 'data', axis=0, tiled=False)]
    pallas_call x1, Pallas kernels: 308 us -> 321 us  [backward_scatter(): pl.pallas_call(functools.partial(bwd_kernel, inv), grid=(UNITS + DEPTH,),...]
    pallas_call x4, Pallas kernels: 216 us -> 206 us  [update_forward(): pl.pallas_call(functools.partial(upd_kernel, lo, hi, nalias), grid=(n,),...]
    pallas_call x1, Pallas kernels: 55.2 us -> 48.3 us  [forward_first(): pl.pallas_call(fwd_kernel, grid=(LAYERS,), in_specs=[full, hbm, hbm], out...]
  transfers between devices with their start and end apart: 3 -> 3, of which waited for: 2 -> 2; matrix products, arithmetic and copies ran while one was open for 0% -> 0% of each run, Pallas kernels for 31% -> 32%
where the time goes in v3:
time: 596 us
  Pallas kernels  576 us (97%)
  between operations  13.8 us (2%)
    pallas_call x1, Pallas kernels, backward_scatter(): pl.pallas_call(functools.partial(bwd_kernel, inv), grid=(UNITS + DEPTH,),...  321 us
    pallas_call x4, Pallas kernels, update_forward(): pl.pallas_call(functools.partial(upd_kernel, lo, hi, nalias), grid=(n,),...  206 us
    pallas_call x1, Pallas kernels, forward_first(): pl.pallas_call(fwd_kernel, grid=(LAYERS,), in_specs=[full, hbm, hbm], out...  48.3 us
  transfers between devices with their start and end apart: 3, of which 2 were waited for; matrix products, arithmetic and copies ran while one was open for 0% of the time, Pallas kernels for 32%

profile of v3, /device:TPU:0, one launch (start us, length us, event | category | flops | bytes accessed | tf_op | source)
XLA Modules:
  0.0 595.7 jit_solution(13976370158079229111)
XLA Ops:
  7.2 0.0 all-gather.7.cloned.1.call-start
  7.2 48.3 %fwd_first.1 = (bf16[16,512,512]{2,1,0:T(8,128)(2,1)}, f32[512,512]{1,0:T(8,128)}) custom-call(bf16[512,512]{1,0:T(8,128)(2,1)} %x_ref.1, f32[16,512,2048]{2,1,0:T(8,128)} %rest_0_.7, f32[16,2048,512]{2,1,0:T(8,128)} %rest_1_.7), custom_call_target="tpu_custom_call" | custom-call | tf_op jit(solution)/shard_map/fwd_first/pallas_call | solution.py:98
  55.5 321.3 %bwd_scatter.1 = (bf16[28,2,512,512]{3,2,1,0:T(8,128)(2,1)}, bf16[20,256,128]{2,1,0:T(8,128)(2,1)}, bf16[12,256,128]{2,1,0:T(8,128)(2,1)}, bf16[4,256,128]{2,1,0:T(8,128)(2,1)}) custom-call(f32[16,512,2048]{2,1,0:T(8,128)} %rest_0_.7, f32[16,2048,512]{2,1,0:T(8,128)} %rest_1_.7, bf16[16,512,512]{2,1,0:T(8,128)(2,1)} %get-tuple-element.32.hb_ref, ...), custom_call_target="tpu_custom_call" | custom-call | tf_op jit(solution)/shard_map/bwd_scatter/pallas_call | solution.py:330
  376.8 0.0 all-gather.7.cloned.1.call-update
  376.8 0.0 all-gather.9.cloned.1.call-start
  376.8 0.7 all-gather.9.cloned.1.call-update
  377.5 0.0 all-gather.11.cloned.1.call-start
  377.6 0.7 all-gather.11.cloned.1.call-update
  378.3 85.9 %upd_fwd.4 = (f32[16,512,2048]{2,1,0:T(8,128)}, f32[16,2048,512]{2,1,0:T(8,128)}, f32[16,512,2048]{2,1,0:T(8,128)}, f32[16,2048,512]{2,1,0:T(8,128)}, f32[512,512]{1,0:T(8,128)}) custom-call(bf16[512,512]{1,0:T(8,128)(2,1)} %h_ref.1, bf16[28,2,512,512]{3,2,1,0:T(8,128)(2,1)} %get-tuple-element.34.g_hbm, f32[16,512,2048]{2,1,0:T(8,128)} %rest_0_.7, ...), custom_call_target="tpu_custom_call" | custom-call | flops 15032385536 | bytes 264241152 | tf_op jit(solution)/shard_map/upd_fwd/pallas_call | solution.py:457
  464.1 1.9 all-gather.7.cloned.1.call-done
  466.0 63.8 %upd_fwd.5 = (f32[16,512,2048]{2,1,0:T(8,128)}, f32[16,2048,512]{2,1,0:T(8,128)}, f32[16,512,2048]{2,1,0:T(8,128)}, f32[16,2048,512]{2,1,0:T(8,128)}, f32[512,512]{1,0:T(8,128)}) custom-call(f32[512,512]{1,0:T(8,128)} %get-tuple-element.35.h_ref, ...), custom_call_target="tpu_custom_call", output_to_operand_aliasing={{0}: (6, {}), {1}: (7, {}), {2}: (8, {}), {3}: (9, {})} | custom-call | flops 10737418240 | bytes 188743680 | tf_op jit(solution)/shard_map/upd_fwd/pallas_call | solution.py:457
  529.8 0.8 all-gather.9.cloned.1.call-done
  530.6 40.4 %upd_fwd.6 = (f32[16,512,2048]{2,1,0:T(8,128)}, f32[16,2048,512]{2,1,0:T(8,128)}, f32[16,512,2048]{2,1,0:T(8,128)}, f32[16,2048,512]{2,1,0:T(8,128)}, f32[512,512]{1,0:T(8,128)}) custom-call(f32[512,512]{1,0:T(8,128)} %get-tuple-element.41.h_ref, ...), custom_call_target="tpu_custom_call", output_to_operand_aliasing={{0}: (6, {}), {1}: (7, {}), {2}: (8, {}), {3}: (9, {})} | custom-call | flops 6442450944 | bytes 113246208 | tf_op jit(solution)/shard_map/upd_fwd/pallas_call | solution.py:457
  571.0 0.0 all-gather.11.cloned.1.call-done
  571.0 0.0 copy-start
  571.0 16.1 %upd_fwd.7 = (f32[16,512,2048]{2,1,0:T(8,128)}, f32[16,2048,512]{2,1,0:T(8,128)}, f32[16,512,2048]{2,1,0:T(8,128)}, f32[16,2048,512]{2,1,0:T(8,128)}, f32[512,512]{1,0:T(8,128)}) custom-call(f32[512,512]{1,0:T(8,128)} %get-tuple-element.47.h_ref, ...), custom_call_target="tpu_custom_call", output_to_operand_aliasing={{0}: (6, {}), {1}: (7, {}), {2}: (8, {}), {3}: (9, {})} | custom-call | flops 2147483648 | bytes 37748736 | tf_op jit(solution)/shard_map/upd_fwd/pallas_call | solution.py:457
  587.1 0.0 copy-done
  587.1 1.4 multiply_reduce_fusion
  588.5 0.6 broadcast_multiply_fusion
Async XLA Ops:
  7.2 458.9 %all-gather.7.cloned.1.call-start = ((), (), s32[]{:S(2)}) async-start(), calls=%async_computation | async-start | bytes 22282240 | tf_op jit(solution)/shard_map/all_gather | solution.py:482
  376.8 153.8 %all-gather.9.cloned.1.call-start = ((), (), s32[]{:S(2)}) async-start(), calls=%async_computation.1 | async-start | bytes 13369344 | tf_op jit(solution)/shard_map/all_gather | solution.py:482
  377.5 193.4 %all-gather.11.cloned.1.call-start = ((), (), s32[]{:S(2)}) async-start(), calls=%async_computation.2 | async-start | bytes 4456448 | tf_op jit(solution)/shard_map/all_gather | solution.py:482
  571.0 16.1 %copy-start = (bf16[512,512]{1,0:T(8,128)(2,1)S(1)}, bf16[512,512]{1,0:T(8,128)(2,1)}, u32[]{:S(2)}) copy-start(bf16[512,512]{1,0:T(8,128)(2,1)} %param.15) | copy-start | bytes 1572868
Sparse Core Ops, SparseCore 0:
  376.9 89.0 all-gather.6
  468.2 62.2 all-gather.8
  532.9 35.0 all-gather.10
